TPU v7x, 32 devices: a whole 2x2x4 slice. The times are simulated.
32 devices in a mesh: exp: 8 (over z, x), dat: 4 (over y, core).
Axes of the slice: x: 2, y: 2, z: 4, core: 2. Of those that a mesh axis runs over, the one named last changes fastest.
Arguments:
- tokens: bfloat16 [4096, 1024], P(('exp', 'dat')), may hold values from -6 to 6
- norm_gain: float32 [1024], replicated, may hold values from 0.25 to 1.75
- router_weight: bfloat16 [1024, 32], P(None, 'exp'), may hold values from -0.1875 to 0.1875
- inner_weight: bfloat16 [32, 1024, 4096], P('exp', None, 'dat'), may hold values from -0.1875 to 0.1875
- outer_weight: bfloat16 [32, 4096, 1024], P('exp', 'dat'), may hold values from -0.09375 to 0.09375
- slot_tokens: int32 [32, 256], P('exp', 'dat'), may hold values from 0 to 4095, as said below
- slot_ids: int32 [4096, 2], P(('exp', 'dat')), may hold values from 0 to 8191, as said below
Outputs:
- mixed: bfloat16 [4096, 1024], P(('exp', 'dat'))
Inputs may be any that keep to these rules, and one draw needn't show every extreme that they name: `slot_tokens`: column c of an expert names only tokens of the devices whose dat index is c // 64; one expert names no token twice. The 256 slots of the experts of one exp index in one dat group name tokens of any one device at most 96 times, exactly 96 times for some devices, and no times for some. Every token is named by exactly 2 slots. slot_ids[t] holds the two slots e * 256 + c with slot_tokens[e, c] = t, the smaller first.
All inputs are finite; a program needn't handle non-finite values.
Results may differ from a plain program's by a relative error of at most 0.0085.
Values may be sent and summed in bfloat16 or wider, within the bound.
A program may use at most 64 MiB of HBM per device.

v0:
```python
import jax
import jax.numpy as jnp
from jax import lax
from jax.sharding import PartitionSpec as P

EPSILON = 1e-06


def normalize(tokens, norm_gain):
    values = tokens.astype(jnp.float32)
    scale = lax.rsqrt(jnp.mean(values * values, axis=-1, keepdims=True) + EPSILON)
    return (values * scale * norm_gain).astype(jnp.bfloat16)


def owner_places(slot_ids, experts_dev, capacity, bucket):
    flat_ids = slot_ids.reshape(-1)
    source = flat_ids // capacity // experts_dev
    before = (source[:, None] == source[None, :]) & (flat_ids[None, :] < flat_ids[:, None])
    ranks_in = jnp.sum(before.astype(jnp.int32), axis=1)
    return (source * bucket + ranks_in).reshape(slot_ids.shape)


def expert_places(token_ids, slot_keys, tok_rows, dat_count, bucket):
    owner_of = token_ids // (tok_rows * dat_count)
    before = (owner_of[:, None] == owner_of[None, :]) & (slot_keys[None, :] < slot_keys[:, None])
    ranks_in = jnp.sum(before.astype(jnp.int32), axis=1)
    return owner_of * bucket + ranks_in


def body(tokens, norm_gain, router_weight, inner_weight, outer_weight, slot_tokens, slot_ids):
    exp_count = lax.axis_size("exp")
    dat_count = lax.axis_size("dat")
    tok_rows, width = tokens.shape
    experts_dev, cap_dev = slot_tokens.shape
    bucket = 6 * tok_rows // exp_count
    normed = normalize(tokens, norm_gain)
    picked = slot_tokens.T.reshape(-1)
    expert_iota = lax.broadcasted_iota(jnp.int32, (cap_dev, experts_dev), 1)
    column_iota = lax.broadcasted_iota(jnp.int32, (cap_dev, experts_dev), 0)
    slot_keys = (expert_iota * cap_dev + column_iota).reshape(-1)
    senders = expert_places(picked, slot_keys, tok_rows, dat_count, bucket)
    receivers = owner_places(slot_ids, experts_dev, cap_dev * dat_count, bucket)
    lookup = jnp.any(
        lax.broadcasted_iota(jnp.int32, (exp_count * bucket, 1, 1), 0) == receivers[None], axis=2
    )
    outgoing = jnp.dot(lookup.astype(jnp.bfloat16), normed, preferred_element_type=jnp.float32)
    outgoing = outgoing.astype(jnp.bfloat16).reshape(exp_count, bucket, width)
    arrived = lax.all_to_all(outgoing, "exp", split_axis=0, concat_axis=0, tiled=True).reshape(
        exp_count * bucket, width
    )
    gathered_rows = jnp.take(arrived, senders, axis=0)
    gathered_rows = gathered_rows.reshape(cap_dev, experts_dev, width)
    gate_score = jax.nn.sigmoid(
        jnp.einsum("ced,de->ce", gathered_rows, router_weight, preferred_element_type=jnp.float32)
    )
    inner = jnp.einsum(
        "ced,edf->cef",
        lax.all_gather(gathered_rows, "dat", axis=0, tiled=True),
        inner_weight,
        preferred_element_type=jnp.float32,
    )
    hidden = jax.nn.relu(inner).astype(jnp.bfloat16)
    expert_out = lax.psum_scatter(
        jnp.einsum("cef,efd->ced", hidden, outer_weight, preferred_element_type=jnp.float32).astype(
            jnp.bfloat16
        ),
        "dat",
        scatter_dimension=0,
        tiled=True,
    ).astype(jnp.float32)
    weighted = (gate_score[:, :, None] * expert_out).astype(jnp.bfloat16).reshape(-1, width)
    placing = lax.broadcasted_iota(jnp.int32, (exp_count * bucket, 1), 0) == senders[None, :]
    returning = jnp.dot(placing.astype(jnp.bfloat16), weighted, preferred_element_type=jnp.float32)
    returning = returning.astype(jnp.bfloat16).reshape(exp_count, bucket, width)
    came_back = lax.all_to_all(returning, "exp", split_axis=0, concat_axis=0, tiled=True).reshape(
        exp_count * bucket, width
    )
    combine_table = jnp.sum(
        (
            lax.broadcasted_iota(jnp.int32, (1, 1, exp_count * bucket), 2) == receivers[:, :, None]
        ).astype(jnp.float32),
        axis=1,
    )
    combined = jnp.dot(
        combine_table.astype(jnp.bfloat16), came_back, preferred_element_type=jnp.float32
    )
    return (tokens.astype(jnp.float32) + combined).astype(jnp.bfloat16)


def solution(mesh):
    in_specs = (
        P(("exp", "dat"), None),
        P(),
        P(None, "exp"),
        P("exp", None, "dat"),
        P("exp", "dat", None),
        P("exp", "dat"),
        P(("exp", "dat"), None),
    )
    out_specs = P(("exp", "dat"), None)
    return jax.shard_map(body, mesh=mesh, in_specs=in_specs, out_specs=out_specs, check_vma=False)
```

profile of v0, /device:TPU:0, one launch (start us, length us, event | category | flops | bytes accessed | tf_op | source)
XLA Modules:
  0.0 179.2 jit_solution(5833611524028004718)
XLA Ops:
  6.5 0.0 copy-start
  6.5 0.8 copy.45
  7.3 0.1 reshape.373
  7.5 0.2 convert_reduce_fusion.2
  7.7 0.1 reduce_sum.43
  7.9 0.1 copy.46
  7.9 0.7 multiply_add_fusion.1
  8.6 0.1 fusion.10
  8.7 1.1 fusion.11
  9.8 0.0 copy-start.3
  9.8 2.8 %convolution_convert_fusion = bf16[768,1024]{1,0:T(8,128)(2,1)} fusion(pred[768,128]{1,0:T(8,128)(4,1)S(1)} %fusion.10, bf16[128,1024]{1,0:T(8,128)(2,1)} %param.7, f32[1024]{0:T(1024)} %param.8, f32[128]{0:T(128)S(1)} %add_rsqrt_fusion), kind=kOutput, calls=%fused_computation.6 | convolution fusion | flops 202637312 | bytes 1937920 | tf_op jit(solution)/shard_map/dot_general | solution.py:46
  12.6 7.3 %all-to-all-start = ((bf16[8,96,1024]{2,1,0:T(8,128)(2,1)}), bf16[8,96,1024]{2,1,0:T(8,128)(2,1)S(1)}, u32[]{:S(2)}, u32[]{:S(2)}) async-start(bf16[8,96,1024]{2,1,0:T(8,128)(2,1)} %bitcast.1), calls=%async_computation | async-start | bytes 3145728 | tf_op jit(solution)/shard_map/all_to_all | solution.py:48
  19.9 0.0 all-gather.2.cloned.1.call-start
  19.9 0.0 copy-done.3
  19.9 0.1 copy.47
  20.0 0.1 reshape.374
  20.1 0.1 reshape.377
  20.3 0.1 add.133
  20.4 0.2 convert_reduce_fusion.1
  20.6 0.1 reduce_sum.46
  20.7 0.1 copy.48
  20.8 0.1 copy.49
  21.0 35.9 %all-to-all-done = bf16[8,96,1024]{2,1,0:T(8,128)(2,1)S(1)} async-done(((bf16[8,96,1024]{2,1,0:T(8,128)(2,1)}), bf16[8,96,1024]{2,1,0:T(8,128)(2,1)S(1)}, u32[]{:S(2)}, u32[]{:S(2)}) %all-to-all-start) | async-done | bytes 1572896 | tf_op jit(solution)/shard_map/all_to_all | solution.py:48
  56.9 1.2 gather_fusion
  58.1 0.2 gather.7
  58.3 1.1 broadcast_select_fusion
  59.4 0.0 all-gather.2.cloned.1.call-update
  59.4 0.0 reduce-scatter.2.cloned.1.call-start
  59.5 21.7 %all-gather.2.cloned.1.call-done = bf16[256,4,1024]{2,1,0:T(4,128)(2,1)} async-done(((bf16[64,4,1024]{2,1,0:T(4,128)(2,1)}), bf16[256,4,1024]{2,1,0:T(4,128)(2,1)}) %all-gather.2.cloned.1.call-update) | async-done | bytes 2097168 | tf_op jit(solution)/shard_map/all_gather | solution.py:58
  81.2 12.8 %convert_bitcast_fusion = bf16[256,4,1024]{2,0,1:T(8,128)(2,1)} fusion(bf16[4,1024,1024]{2,1,0:T(8,128)(2,1)} %param.11, bf16[4,1024,1024]{2,1,0:T(8,128)(2,1)} %param.10, bf16[256,4,1024]{2,1,0:T(4,128)(2,1)} %all-gather.2.cloned.1.call-done), kind=kOutput, calls=%fused_computation.5 | convolution fusion | flops 4298113024 | bytes 20971520 | tf_op jit(solution)/shard_map/cef,efd->ced/dot_general | solution.py:64
  94.0 0.0 copy-start.2
  94.0 0.0 reduce-scatter.2.cloned.1.call-update
  94.0 0.0 copy-done
  94.0 1.0 copy-done.2
  95.0 0.3 fusion.14
  95.3 30.1 %reduce-scatter.2.cloned.1.call-done = bf16[64,4,1024]{2,0,1:T(8,128)(2,1)} async-done(((bf16[256,4,1024]{2,0,1:T(8,128)(2,1)}), bf16[64,4,1024]{2,0,1:T(8,128)(2,1)}) %reduce-scatter.2.cloned.1.call-update) | async-done | bytes 524304 | tf_op jit(solution)/shard_map/reduce_scatter | solution.py:63
  125.3 1.2 multiply_convert_fusion
  126.5 0.4 copy.52
  127.0 0.1 reshape.378
  127.1 1.7 convolution_convert_fusion.1
  128.8 0.0 copy-start.1
  128.8 5.6 %all-to-all-start.1 = ((bf16[8,96,1024]{2,1,0:T(8,128)(2,1)}), bf16[8,96,1024]{2,1,0:T(8,128)(2,1)S(1)}, u32[]{:S(2)}, u32[]{:S(2)}) async-start(bf16[8,96,1024]{2,1,0:T(8,128)(2,1)} %bitcast.11), calls=%async_computation.2 | async-start | bytes 3145728 | tf_op jit(solution)/shard_map/all_to_all | solution.py:75
  134.5 0.1 convert_reduce_fusion
  134.6 36.7 %all-to-all-done.1 = bf16[8,96,1024]{2,1,0:T(8,128)(2,1)S(1)} async-done(((bf16[8,96,1024]{2,1,0:T(8,128)(2,1)}), bf16[8,96,1024]{2,1,0:T(8,128)(2,1)S(1)}, u32[]{:S(2)}, u32[]{:S(2)}) %all-to-all-start.1) | async-done | bytes 1572896 | tf_op jit(solution)/shard_map/all_to_all | solution.py:75
  171.3 0.0 copy-done.1
  171.3 1.1 fusion.5
  (10 shorter events, 0.1 us)
Async XLA Ops:
  6.5 87.5 %copy-start = (bf16[1024,4]{0,1:T(4,128)(2,1)S(1)}, bf16[1024,4]{0,1:T(4,128)(2,1)}, u32[]{:S(2)}) copy-start(bf16[1024,4]{0,1:T(4,128)(2,1)} %param.9) | copy-start | bytes 24580
  9.8 10.1 %copy-start.3 = (s32[4,64]{1,0:T(4,128)S(1)}, s32[4,64]{1,0:T(4,128)}, u32[]{:S(2)}) copy-start(s32[4,64]{1,0:T(4,128)} %param.12) | copy-start | bytes 3076
  12.6 44.3 %all-to-all-start = ((bf16[8,96,1024]{2,1,0:T(8,128)(2,1)}), bf16[8,96,1024]{2,1,0:T(8,128)(2,1)S(1)}, u32[]{:S(2)}, u32[]{:S(2)}) async-start(bf16[8,96,1024]{2,1,0:T(8,128)(2,1)} %bitcast.1), calls=%async_computation | async-start | bytes 3145728 | tf_op jit(solution)/shard_map/all_to_all | solution.py:48
  19.9 61.3 %all-gather.2.cloned.1.call-start = ((), (), s32[]{:S(2)}) async-start(), calls=%async_computation.3 | async-start | bytes 2621440 | tf_op jit(solution)/shard_map/all_gather | solution.py:58
  59.4 65.9 %reduce-scatter.2.cloned.1.call-start = ((), (), s32[]{:S(2)}) async-start(), calls=%async_computation.4 | async-start | bytes 2621440 | tf_op jit(solution)/shard_map/reduce_scatter | solution.py:63
  94.0 1.0 copy-start.2
  128.8 42.5 %copy-start.1 = (bf16[128,1024]{1,0:T(8,128)(2,1)S(1)}, bf16[128,1024]{1,0:T(8,128)(2,1)}, u32[]{:S(2)}) copy-start(bf16[128,1024]{1,0:T(8,128)(2,1)} %param.7) | copy-start | bytes 786436
  128.8 42.5 %all-to-all-start.1 = ((bf16[8,96,1024]{2,1,0:T(8,128)(2,1)}), bf16[8,96,1024]{2,1,0:T(8,128)(2,1)S(1)}, u32[]{:S(2)}, u32[]{:S(2)}) async-start(bf16[8,96,1024]{2,1,0:T(8,128)(2,1)} %bitcast.11), calls=%async_computation.2 | async-start | bytes 3145728 | tf_op jit(solution)/shard_map/all_to_all | solution.py:75
Sparse Core Ops, SparseCore 0:
  59.5 21.6 all-gather.1
  94.1 31.1 reduce-scatter.1
where the time goes:
time: 180 us; the launch traced here: 179 us
  waiting for transfers between devices  124 us (69%)
  matrix products  18.6 us (10%)
  between operations  13.6 us (8%)
  starting transfers between devices  13 us (7%)
  other arithmetic  4.88 us (3%)
  local copies, waits for them, and re-layouts  4.73 us (3%)
    all_to_all x1, waiting for transfers between devices, body(): lax.all_to_all(returning, 'exp', split_axis=0, concat_axis=0, tiled=True)  36.7 us
    all_to_all x1, waiting for transfers between devices, body(): lax.all_to_all(outgoing, 'exp', split_axis=0, concat_axis=0, tiled=True)  35.9 us
    reduce_scatter x1, waiting for transfers between devices, body(): lax.psum_scatter(jnp.einsum('cef,efd->ced', hidden, outer_weight, preferr...  30.1 us
    all_gather x1, waiting for transfers between devices, body(): lax.all_gather(gathered_rows, 'dat', axis=0, tiled=True)  21.7 us
    dot_general x1, matrix products, body(): jnp.einsum('cef,efd->ced', hidden, outer_weight, preferred_element_type=j...  12.8 us
    all_to_all x1, starting transfers between devices, body(): lax.all_to_all(outgoing, 'exp', split_axis=0, concat_axis=0, tiled=True)  7.28 us
    all_to_all x1, starting transfers between devices, body(): lax.all_to_all(returning, 'exp', split_axis=0, concat_axis=0, tiled=True)  5.64 us
  transfers between devices with their start and end apart: 4, of which 4 were waited for; matrix products, arithmetic and copies ran while one was open for 1% of the time, Pallas kernels for 0%

commit v1 on v0

--- a/solution.py
+++ b/solution.py
@@ -1,6 +1,8 @@
 import jax
 import jax.numpy as jnp
 from jax import lax
+from jax.experimental import pallas as pl
+from jax.experimental.pallas import tpu as pltpu
 from jax.sharding import PartitionSpec as P
 
 EPSILON = 1e-06
@@ -87,7 +89,314 @@
     return (tokens.astype(jnp.float32) + combined).astype(jnp.bfloat16)
 
 
+MESH = pl.DeviceIdType.MESH
+PAIR = 2
+CHUNK = 256
+
+
+def moe_kernel(
+    tokens_ref, gain_ref, router_ref, ids_ref, inner_hbm, outer_hbm, out_ref,
+    inner_v, outer_v, ids_far, pick, place, blocks, own_part, far_send, far_recv,
+    rows, hidden, gate, parts, core_recv, y_send, y_recv, kept, weighted, x_recv,
+    dense, up_send, up_recv, down_send, down_recv,
+    w_sem, ids_sem, zu_sem, zd_sem, x_sem, y_sem, c_sem, cr_sem,
+    rc_sem, ry_sem, rx_sem, ru_sem, rd_sem,
+):
+    chunks, lines, tok_rows, wide = blocks.shape
+    experts_dev = inner_v.shape[0]
+    slots = weighted.shape[1]
+    cap_dev = slots // experts_dev
+    exp = lax.axis_index("exp")
+    dat = lax.axis_index("dat")
+    dat_count = lax.axis_size("dat")
+    z, x = exp // PAIR, exp % PAIR
+    y, c = dat // PAIR, dat % PAIR
+    up = (exp + PAIR, dat)
+    down = (exp - PAIR, dat)
+    x_peer = (exp + 1 - 2 * x, dat)
+    y_peer = (exp, dat + PAIR - 2 * PAIR * y)
+    c_peer = (exp, dat + 1 - 2 * c)
+    has_up = z + 1 < lines
+    has_down = z > 0
+    sent = []
+
+    def copy_to(src, dst, sems, where, peer):
+        return pltpu.make_async_remote_copy(
+            src_ref=src, dst_ref=dst, send_sem=sems.at[(0,) + where],
+            recv_sem=sems.at[(1,) + where], device_id=peer, device_id_type=MESH,
+        )
+
+    def send(copy, cond=None):
+        sent.append((copy, cond))
+        if cond is None:
+            copy.start()
+        else:
+            pl.when(cond)(copy.start)
+
+    loads = []
+    for e in range(experts_dev):
+        loads.append(pltpu.make_async_copy(inner_hbm.at[e], inner_v.at[e], w_sem.at[0, e]))
+    for e in range(experts_dev):
+        loads.append(pltpu.make_async_copy(outer_hbm.at[e], outer_v.at[e], w_sem.at[1, e]))
+    for load in loads:
+        load.start()
+
+    barrier = pltpu.get_barrier_semaphore()
+    for peer in (x_peer, y_peer, c_peer):
+        pl.semaphore_signal(barrier, inc=1, device_id=peer, device_id_type=MESH)
+
+    @pl.when(has_up)
+    def _():
+        pl.semaphore_signal(barrier, inc=1, device_id=up, device_id_type=MESH)
+
+    @pl.when(has_down)
+    def _():
+        pl.semaphore_signal(barrier, inc=1, device_id=down, device_id_type=MESH)
+
+    values = tokens_ref[...].astype(jnp.float32)
+    scale = lax.rsqrt(jnp.mean(values * values, axis=-1, keepdims=True) + EPSILON)
+    normed = (values * scale * gain_ref[...]).astype(jnp.bfloat16)
+    for j in range(chunks):
+        blocks[j, z] = normed[:, j * wide : (j + 1) * wide]
+
+    pl.semaphore_wait(barrier, 3 + has_up.astype(jnp.int32) + has_down.astype(jnp.int32))
+
+    ids_copy = copy_to(ids_ref, ids_far, ids_sem, (), x_peer)
+
+    def one_hots(side, ids):
+        for s in range(lines):
+            base = ((s * PAIR + x) * dat_count + dat) * tok_rows
+            local = lax.broadcasted_iota(jnp.int32, (tok_rows, slots), 0) + base
+            hot = (ids[0:1, :] == local).astype(jnp.float32)
+            place[side, s * tok_rows : (s + 1) * tok_rows, :] = hot.astype(jnp.bfloat16)
+            pick[side, :, s * tok_rows : (s + 1) * tok_rows] = hot.T.astype(jnp.bfloat16)
+
+    def own_rows(j, of_dat):
+        return rows.at[j, :, pl.ds(pl.multiple_of(of_dat * cap_dev, cap_dev), cap_dev), :]
+
+    dat_y = dat + PAIR - 2 * PAIR * y
+    dat_c = dat + 1 - 2 * c
+    dat_yc = dat_y + 1 - 2 * c
+
+    for t in range(chunks + lines + 2):
+        if t < chunks:
+            send(copy_to(blocks.at[t, z], blocks.at[t, z], zu_sem, (t, z), up), has_up)
+            send(copy_to(blocks.at[t, z], blocks.at[t, z], zd_sem, (t, z), down), has_down)
+        if t == 0:
+            send(ids_copy)
+            one_hots(0, ids_ref)
+        if t == 1:
+            ids_copy.wait_recv()
+            one_hots(1, ids_far)
+        for k in range(1, lines):
+            j = t - k
+            if 0 <= j < chunks:
+                low, high = z - k, z + k
+                from_low = copy_to(blocks.at[j, low], blocks.at[j, low], zu_sem, (j, low), up)
+                from_high = copy_to(blocks.at[j, high], blocks.at[j, high], zd_sem, (j, high), down)
+                pl.when(low >= 0)(from_low.wait_recv)
+                if k + 1 < lines:
+                    send(from_low, (low >= 0) & has_up)
+                pl.when(high < lines)(from_high.wait_recv)
+                if k + 1 < lines:
+                    send(from_high, (high < lines) & has_down)
+        j = t - (lines - 1)
+        if 0 <= j < chunks:
+            found = blocks[j].reshape(lines * tok_rows, wide)
+            far_send[j] = jnp.dot(pick[1], found, preferred_element_type=jnp.float32).astype(jnp.bfloat16)
+            send(copy_to(far_send.at[j], far_recv.at[j], x_sem, (j,), x_peer))
+            own_part[j] = jnp.dot(pick[0], found, preferred_element_type=jnp.float32)
+        j = t - lines
+        if 0 <= j < chunks:
+            copy_to(far_send.at[j], far_recv.at[j], x_sem, (j,), x_peer).wait_recv()
+            merged = (own_part[j] + far_recv[j].astype(jnp.float32)).astype(jnp.bfloat16)
+            own_rows(j, dat)[...] = merged.reshape(experts_dev, cap_dev, wide)
+            send(copy_to(own_rows(j, dat), own_rows(j, dat), y_sem, (j,), y_peer))
+            send(copy_to(own_rows(j, dat), own_rows(j, dat), c_sem, (j,), c_peer))
+            score = jnp.dot(
+                merged, router_ref[j * wide : (j + 1) * wide, :], preferred_element_type=jnp.float32
+            )
+            row_id = lax.broadcasted_iota(jnp.int32, score.shape, 0)
+            first = lax.broadcasted_iota(jnp.int32, score.shape, 1) * cap_dev
+            mine = (row_id >= first) & (row_id < first + cap_dev)
+            score = jnp.sum(jnp.where(mine, score, 0.0), axis=1, keepdims=True)
+            gate[...] = score if j == 0 else gate[...] + score
+        j = t - lines - 1
+        if 0 <= j < chunks:
+            copy_to(own_rows(j, dat_y), own_rows(j, dat_y), y_sem, (j,), y_peer).wait_recv()
+            send(copy_to(own_rows(j, dat_y), own_rows(j, dat_y), cr_sem, (j,), c_peer))
+    gate[...] = jax.nn.sigmoid(gate[...])
+    for j in range(chunks):
+        copy_to(own_rows(j, dat_c), own_rows(j, dat_c), c_sem, (j,), c_peer).wait_recv()
+        copy_to(own_rows(j, dat_yc), own_rows(j, dat_yc), cr_sem, (j,), c_peer).wait_recv()
+    for load in loads:
+        load.wait()
+
+    @pl.loop(0, experts_dev)
+    def _(e):
+        total = jnp.dot(rows[0, e], inner_v[e, :wide, :], preferred_element_type=jnp.float32)
+        for j in range(1, chunks):
+            total += jnp.dot(
+                rows[j, e], inner_v[e, j * wide : (j + 1) * wide, :], preferred_element_type=jnp.float32
+            )
+        hidden[e] = jnp.maximum(total, 0.0).astype(jnp.bfloat16)
+
+    def block(s):
+        return slice(s * tok_rows, (s + 1) * tok_rows)
+
+    for t in range(chunks + 4 + lines):
+        j = t
+        if j < chunks:
+
+            @pl.loop(0, experts_dev)
+            def _(e, j=j):
+                part = jnp.dot(
+                    hidden[e], outer_v[e, :, j * wide : (j + 1) * wide], preferred_element_type=jnp.float32
+                ).astype(jnp.bfloat16)
+                for d in range(PAIR * PAIR):
+                    parts[j, d // PAIR, d % PAIR, e] = part[d * cap_dev : (d + 1) * cap_dev, :]
+
+            send(copy_to(parts.at[j, :, 1 - c], core_recv.at[j], rc_sem, (j,), c_peer))
+        j = t - 1
+        if 0 <= j < chunks:
+            copy_to(parts.at[j, :, 1 - c], core_recv.at[j], rc_sem, (j,), c_peer).wait_recv()
+            theirs = parts[j, 1 - y, c].astype(jnp.float32) + core_recv[j, 1 - y].astype(jnp.float32)
+            y_send[j] = theirs.astype(jnp.bfloat16).reshape(slots, wide)
+            send(copy_to(y_send.at[j], y_recv.at[j], ry_sem, (j,), y_peer))
+            ours = parts[j, y, c].astype(jnp.float32) + core_recv[j, y].astype(jnp.float32)
+            kept[j] = ours.reshape(slots, wide)
+        j = t - 2
+        if 0 <= j < chunks:
+            copy_to(y_send.at[j], y_recv.at[j], ry_sem, (j,), y_peer).wait_recv()
+            summed = kept[j] + y_recv[j].astype(jnp.float32)
+            weighted[j] = (gate[...] * summed).astype(jnp.bfloat16)
+            send(copy_to(weighted.at[j], x_recv.at[j], rx_sem, (j,), x_peer))
+        j = t - 3
+        if 0 <= j < chunks:
+            copy_to(weighted.at[j], x_recv.at[j], rx_sem, (j,), x_peer).wait_recv()
+            spread = jnp.dot(place[0], weighted[j], preferred_element_type=jnp.float32)
+            spread += jnp.dot(place[1], x_recv[j], preferred_element_type=jnp.float32)
+            dense[j] = spread
+        for s in range(lines):
+            j = t - 3 - s
+            if not 0 <= j < chunks:
+                continue
+            for dest in range(lines - 1, s, -1):
+                here = z == s
+                go = copy_to(up_send.at[j, dest], up_recv.at[j, dest], ru_sem, (j, dest), up)
+
+                @pl.when(here)
+                def _(j=j, dest=dest, s=s, go=go):
+                    total = dense[j, block(dest), :]
+                    if s > 0:
+                        go.wait_recv()
+                        total += up_recv[j, dest].astype(jnp.float32)
+                    up_send[j, dest] = total.astype(jnp.bfloat16)
+
+                send(go, here)
+            top = lines - 1 - s
+            for dest in range(top):
+                here = z == top
+                go = copy_to(down_send.at[j, dest], down_recv.at[j, dest], rd_sem, (j, dest), down)
+
+                @pl.when(here)
+                def _(j=j, dest=dest, top=top, go=go):
+                    total = dense[j, block(dest), :]
+                    if top < lines - 1:
+                        go.wait_recv()
+                        total += down_recv[j, dest].astype(jnp.float32)
+                    down_send[j, dest] = total.astype(jnp.bfloat16)
+
+                send(go, here)
+        j = t - 3 - lines
+        if 0 <= j < chunks:
+            for s in range(lines):
+
+                @pl.when(z == s)
+                def _(j=j, s=s):
+                    cols = slice(j * wide, (j + 1) * wide)
+                    total = dense[j, block(s), :]
+                    if s > 0:
+                        copy_to(up_send.at[j, s], up_recv.at[j, s], ru_sem, (j, s), up).wait_recv()
+                        total += up_recv[j, s].astype(jnp.float32)
+                    if s < lines - 1:
+                        copy_to(down_send.at[j, s], down_recv.at[j, s], rd_sem, (j, s), down).wait_recv()
+                        total += down_recv[j, s].astype(jnp.float32)
+                    out_ref[:, cols] = (tokens_ref[:, cols].astype(jnp.float32) + total).astype(jnp.bfloat16)
+
+    for copy, cond in sent:
+        if cond is None:
+            copy.wait_send()
+        else:
+            pl.when(cond)(copy.wait_send)
+
+
+def kernel_body(tokens, norm_gain, router_weight, inner_weight, outer_weight, slot_tokens, slot_ids):
+    del slot_ids
+    tok_rows, width = tokens.shape
+    experts_dev, cap_dev = slot_tokens.shape
+    units = inner_weight.shape[2]
+    lines = lax.axis_size("exp") // PAIR
+    dat_count = lax.axis_size("dat")
+    slots = experts_dev * cap_dev
+    chunks = width // CHUNK
+    ids = jnp.broadcast_to(slot_tokens.reshape(1, slots), (8, slots))
+    bf16, f32 = jnp.bfloat16, jnp.float32
+    vmem = pl.BlockSpec(memory_space=pltpu.VMEM)
+    hbm = pl.BlockSpec(memory_space=pl.ANY)
+    dma = pltpu.SemaphoreType.DMA
+    return pl.pallas_call(
+        moe_kernel,
+        out_shape=jax.ShapeDtypeStruct((tok_rows, width), bf16),
+        in_specs=[vmem, vmem, vmem, vmem, hbm, hbm],
+        out_specs=vmem,
+        scratch_shapes=[
+            pltpu.VMEM((experts_dev, width, units), bf16),
+            pltpu.VMEM((experts_dev, units, width), bf16),
+            pltpu.VMEM((8, slots), jnp.int32),
+            pltpu.VMEM((2, slots, lines * tok_rows), bf16),
+            pltpu.VMEM((2, lines * tok_rows, slots), bf16),
+            pltpu.VMEM((chunks, lines, tok_rows, CHUNK), bf16),
+            pltpu.VMEM((chunks, slots, CHUNK), f32),
+            pltpu.VMEM((chunks, slots, CHUNK), bf16),
+            pltpu.VMEM((chunks, slots, CHUNK), bf16),
+            pltpu.VMEM((chunks, experts_dev, dat_count * cap_dev, CHUNK), bf16),
+            pltpu.VMEM((experts_dev, dat_count * cap_dev, units), bf16),
+            pltpu.VMEM((slots, 1), f32),
+            pltpu.VMEM((chunks, PAIR, PAIR, experts_dev, cap_dev, CHUNK), bf16),
+            pltpu.VMEM((chunks, PAIR, experts_dev, cap_dev, CHUNK), bf16),
+            pltpu.VMEM((chunks, slots, CHUNK), bf16),
+            pltpu.VMEM((chunks, slots, CHUNK), bf16),
+            pltpu.VMEM((chunks, slots, CHUNK), f32),
+            pltpu.VMEM((chunks, slots, CHUNK), bf16),
+            pltpu.VMEM((chunks, slots, CHUNK), bf16),
+            pltpu.VMEM((chunks, lines * tok_rows, CHUNK), f32),
+            pltpu.VMEM((chunks, lines, tok_rows, CHUNK), bf16),
+            pltpu.VMEM((chunks, lines, tok_rows, CHUNK), bf16),
+            pltpu.VMEM((chunks, lines, tok_rows, CHUNK), bf16),
+            pltpu.VMEM((chunks, lines, tok_rows, CHUNK), bf16),
+            dma((2, experts_dev)),
+            dma((2,)),
+            dma((2, chunks, lines)),
+            dma((2, chunks, lines)),
+            dma((2, chunks)),
+            dma((2, chunks)),
+            dma((2, chunks)),
+            dma((2, chunks)),
+            dma((2, chunks)),
+            dma((2, chunks)),
+            dma((2, chunks)),
+            dma((2, chunks, lines)),
+            dma((2, chunks, lines)),
+        ],
+        compiler_params=pltpu.CompilerParams(
+            collective_id=0, has_side_effects=True, vmem_limit_bytes=60 * 1024 * 1024
+        ),
+    )(tokens, norm_gain.reshape(1, width), router_weight, ids, inner_weight, outer_weight)
+
+
 def solution(mesh):
+    chosen = kernel_body if mesh.shape["dat"] == PAIR * PAIR else body
     in_specs = (
         P(("exp", "dat"), None),
         P(),
@@ -98,4 +407,4 @@
         P(("exp", "dat"), None),
     )
     out_specs = P(("exp", "dat"), None)
-    return jax.shard_map(body, mesh=mesh, in_specs=in_specs, out_specs=out_specs, check_vma=False)
+    return jax.shard_map(chosen, mesh=mesh, in_specs=in_specs, out_specs=out_specs, check_vma=False)

time: 180 us -> 82.8 us (0.46)
  waiting for transfers between devices: 124 us -> 0 us
  Pallas kernels: 0 us -> 77.9 us
  matrix products: 18.6 us -> 0 us
  between operations: 13.6 us -> 0.01 us
  starting transfers between devices: 13 us -> 0 us
  other arithmetic: 4.88 us -> 0 us
    pallas_call x0 -> x1, Pallas kernels: none -> 77.9 us  [kernel_body(): pl.pallas_call(moe_kernel, out_shape=jax.ShapeDtypeStruct((tok_rows, widt...]
    all_to_all x2 -> x0, waiting for transfers between devices: 72.6 us -> none  [the longest x1 36.7 us: body(): lax.all_to_all(returning, 'exp', split_axis=0, concat_axis=0, tiled=True)]
    reduce_scatter x1 -> x0, waiting for transfers between devices: 30.1 us -> none  [body(): lax.psum_scatter(jnp.einsum('cef,efd->ced', hidden, outer_weight, preferr...]
    all_gather x1 -> x0, waiting for transfers between devices: 21.7 us -> none  [body(): lax.all_gather(gathered_rows, 'dat', axis=0, tiled=True)]
    dot_general x5 -> x0, matrix products: 18.6 us -> none  [the longest x1 12.8 us: body(): jnp.einsum('cef,efd->ced', hidden, outer_weight, preferred_element_type=j...]
    all_to_all x2 -> x0, starting transfers between devices: 12.9 us -> none  [the longest x1 7.28 us: body(): lax.all_to_all(outgoing, 'exp', split_axis=0, concat_axis=0, tiled=True)]
  transfers between devices with their start and end apart: 4 -> 0, of which waited for: 4 -> 0; matrix products, arithmetic and copies ran while one was open for 1% -> 0% of each run, Pallas kernels for 0% -> 0%
where the time goes in v1:
time: 82.8 us; the launch traced here: 82.5 us
  Pallas kernels  77.9 us (94%)
  local copies, waits for them, and re-layouts  4.6 us (6%)
    pallas_call x1, Pallas kernels, kernel_body(): pl.pallas_call(moe_kernel, out_shape=jax.ShapeDtypeStruct((tok_rows, widt...  77.9 us
    unnamed x2, local copies, waits for them, and re-layouts  3.25 us

profile of v1, /device:TPU:0, one launch (start us, length us, event | category | flops | bytes accessed | tf_op | source)
XLA Modules:
  0.0 82.5 jit_solution(4317978330098256571)
XLA Ops:
  0.0 0.8 broadcast_in_dim.7
  0.8 0.6 broadcast_in_dim.8.ids_ref
  1.4 1.6 %copy.7.router_ref = bf16[1024,4]{1,0:T(8,128)(2,1)} copy(bf16[1024,4]{0,1:T(4,128)(2,1)} %param.9) | data formatting | bytes 16384 | tf_op args[2]
  2.9 77.9 %shard_map.64 = bf16[128,1024]{1,0:T(8,128)(2,1)} custom-call(bf16[128,1024]{1,0:T(8,128)(2,1)} %tokens_ref.1, f32[1,1024]{1,0:T(1,128)} %bitcast.1, bf16[1024,4]{1,0:T(8,128)(2,1)} %copy.7.router_ref, s32[8,256]{1,0:T(8,128)} %broadcast_in_dim.8.ids_ref, bf16[4,1024,1024]{2,1,0:T(8,128)(2,1)} %inner_hbm.1, bf16[4,1024,1024]{2,1,0:T(8,128)(2,1)} %outer_hbm.1), custom_call_target="tpu_custom_call" | custom-call | tf_op jit(solution)/shard_map/pallas_call | solution.py:348
  80.9 1.7 %copy.9 = bf16[128,1024]{1,0:T(8,128)(2,1)} copy(bf16[128,1024]{1,0:T(8,128)(2,1)} %shard_map.64) | data formatting | bytes 524288

commit v2 on v1

--- a/solution.py
+++ b/solution.py
@@ -92,12 +92,13 @@
 MESH = pl.DeviceIdType.MESH
 PAIR = 2
 CHUNK = 256
+GROUP = 256
 
 
 def moe_kernel(
     tokens_ref, gain_ref, router_ref, ids_ref, inner_hbm, outer_hbm, out_ref,
     inner_v, outer_v, ids_far, pick, place, blocks, own_part, far_send, far_recv,
-    rows, hidden, gate, parts, core_recv, y_send, y_recv, kept, weighted, x_recv,
+    rows, sums, hidden, gate, parts, core_recv, y_send, y_recv, kept, weighted, x_recv,
     dense, up_send, up_recv, down_send, down_recv,
     w_sem, ids_sem, zu_sem, zd_sem, x_sem, y_sem, c_sem, cr_sem,
     rc_sem, ry_sem, rx_sem, ru_sem, rd_sem,
@@ -105,6 +106,8 @@
     chunks, lines, tok_rows, wide = blocks.shape
     experts_dev = inner_v.shape[0]
     slots = weighted.shape[1]
+    groups, span = rows.shape[0], rows.shape[3]
+    per = span // wide
     cap_dev = slots // experts_dev
     exp = lax.axis_index("exp")
     dat = lax.axis_index("dat")
@@ -167,18 +170,38 @@
         for s in range(lines):
             base = ((s * PAIR + x) * dat_count + dat) * tok_rows
             local = lax.broadcasted_iota(jnp.int32, (tok_rows, slots), 0) + base
-            hot = (ids[0:1, :] == local).astype(jnp.float32)
+            all_ids = jnp.concatenate([ids[e : e + 1, :] for e in range(experts_dev)], axis=1)
+            hot = (all_ids == local).astype(jnp.float32)
             place[side, s * tok_rows : (s + 1) * tok_rows, :] = hot.astype(jnp.bfloat16)
             pick[side, :, s * tok_rows : (s + 1) * tok_rows] = hot.T.astype(jnp.bfloat16)
 
     def own_rows(j, of_dat):
-        return rows.at[j, :, pl.ds(pl.multiple_of(of_dat * cap_dev, cap_dev), cap_dev), :]
+        first = (j % per) * wide
+        at = pl.ds(pl.multiple_of(of_dat * cap_dev, cap_dev), cap_dev)
+        return rows.at[j // per, :, at, first : first + wide]
+
+    def first_product(g):
+        if g == 0:
+            for e in range(experts_dev):
+                loads[e].wait()
+
+        @pl.loop(0, experts_dev, unroll=True)
+        def _(e):
+            total = jnp.dot(
+                rows[g, e], inner_v[e, g * span : (g + 1) * span, :], preferred_element_type=jnp.float32
+            )
+            if g > 0:
+                total += sums[e]
+            if g + 1 < groups:
+                sums[e] = total
+            else:
+                hidden[e] = jnp.maximum(total, 0.0).astype(jnp.bfloat16)
 
     dat_y = dat + PAIR - 2 * PAIR * y
     dat_c = dat + 1 - 2 * c
     dat_yc = dat_y + 1 - 2 * c
 
-    for t in range(chunks + lines + 2):
+    for t in range(chunks + lines + 3):
         if t < chunks:
             send(copy_to(blocks.at[t, z], blocks.at[t, z], zu_sem, (t, z), up), has_up)
             send(copy_to(blocks.at[t, z], blocks.at[t, z], zd_sem, (t, z), down), has_down)
@@ -213,8 +236,9 @@
             own_rows(j, dat)[...] = merged.reshape(experts_dev, cap_dev, wide)
             send(copy_to(own_rows(j, dat), own_rows(j, dat), y_sem, (j,), y_peer))
             send(copy_to(own_rows(j, dat), own_rows(j, dat), c_sem, (j,), c_peer))
-            score = jnp.dot(
-                merged, router_ref[j * wide : (j + 1) * wide, :], preferred_element_type=jnp.float32
+            score = lax.dot_general(
+                merged, router_ref[:, j * wide : (j + 1) * wide], (((1,), (1,)), ((), ())),
+                preferred_element_type=jnp.float32,
             )
             row_id = lax.broadcasted_iota(jnp.int32, score.shape, 0)
             first = lax.broadcasted_iota(jnp.int32, score.shape, 1) * cap_dev
@@ -225,21 +249,15 @@
         if 0 <= j < chunks:
             copy_to(own_rows(j, dat_y), own_rows(j, dat_y), y_sem, (j,), y_peer).wait_recv()
             send(copy_to(own_rows(j, dat_y), own_rows(j, dat_y), cr_sem, (j,), c_peer))
+        j = t - lines - 2
+        if 0 <= j < chunks:
+            copy_to(own_rows(j, dat_c), own_rows(j, dat_c), c_sem, (j,), c_peer).wait_recv()
+            copy_to(own_rows(j, dat_yc), own_rows(j, dat_yc), cr_sem, (j,), c_peer).wait_recv()
+            if (j + 1) % per == 0:
+                first_product(j // per)
     gate[...] = jax.nn.sigmoid(gate[...])
-    for j in range(chunks):
-        copy_to(own_rows(j, dat_c), own_rows(j, dat_c), c_sem, (j,), c_peer).wait_recv()
-        copy_to(own_rows(j, dat_yc), own_rows(j, dat_yc), cr_sem, (j,), c_peer).wait_recv()
-    for load in loads:
-        load.wait()
-
-    @pl.loop(0, experts_dev)
-    def _(e):
-        total = jnp.dot(rows[0, e], inner_v[e, :wide, :], preferred_element_type=jnp.float32)
-        for j in range(1, chunks):
-            total += jnp.dot(
-                rows[j, e], inner_v[e, j * wide : (j + 1) * wide, :], preferred_element_type=jnp.float32
-            )
-        hidden[e] = jnp.maximum(total, 0.0).astype(jnp.bfloat16)
+    for e in range(experts_dev):
+        loads[experts_dev + e].wait()
 
     def block(s):
         return slice(s * tok_rows, (s + 1) * tok_rows)
@@ -247,14 +265,18 @@
     for t in range(chunks + 4 + lines):
         j = t
         if j < chunks:
-
-            @pl.loop(0, experts_dev)
-            def _(e, j=j):
-                part = jnp.dot(
-                    hidden[e], outer_v[e, :, j * wide : (j + 1) * wide], preferred_element_type=jnp.float32
-                ).astype(jnp.bfloat16)
-                for d in range(PAIR * PAIR):
-                    parts[j, d // PAIR, d % PAIR, e] = part[d * cap_dev : (d + 1) * cap_dev, :]
+            if j % per == 0:
+
+                @pl.loop(0, experts_dev, unroll=True)
+                def _(e, j=j):
+                    part = jnp.dot(
+                        hidden[e], outer_v[e, :, j * wide : j * wide + span], preferred_element_type=jnp.float32
+                    ).astype(jnp.bfloat16)
+                    for d in range(PAIR * PAIR):
+                        for k in range(per):
+                            parts[j + k, d // PAIR, d % PAIR, e] = part[
+                                d * cap_dev : (d + 1) * cap_dev, k * wide : (k + 1) * wide
+                            ]
 
             send(copy_to(parts.at[j, :, 1 - c], core_recv.at[j], rc_sem, (j,), c_peer))
         j = t - 1
@@ -340,7 +362,6 @@
     dat_count = lax.axis_size("dat")
     slots = experts_dev * cap_dev
     chunks = width // CHUNK
-    ids = jnp.broadcast_to(slot_tokens.reshape(1, slots), (8, slots))
     bf16, f32 = jnp.bfloat16, jnp.float32
     vmem = pl.BlockSpec(memory_space=pltpu.VMEM)
     hbm = pl.BlockSpec(memory_space=pl.ANY)
@@ -353,14 +374,15 @@
         scratch_shapes=[
             pltpu.VMEM((experts_dev, width, units), bf16),
             pltpu.VMEM((experts_dev, units, width), bf16),
-            pltpu.VMEM((8, slots), jnp.int32),
+            pltpu.VMEM((experts_dev, cap_dev), jnp.int32),
             pltpu.VMEM((2, slots, lines * tok_rows), bf16),
             pltpu.VMEM((2, lines * tok_rows, slots), bf16),
             pltpu.VMEM((chunks, lines, tok_rows, CHUNK), bf16),
             pltpu.VMEM((chunks, slots, CHUNK), f32),
             pltpu.VMEM((chunks, slots, CHUNK), bf16),
             pltpu.VMEM((chunks, slots, CHUNK), bf16),
-            pltpu.VMEM((chunks, experts_dev, dat_count * cap_dev, CHUNK), bf16),
+            pltpu.VMEM((width // GROUP, experts_dev, dat_count * cap_dev, GROUP), bf16),
+            pltpu.VMEM((experts_dev, dat_count * cap_dev, units), f32),
             pltpu.VMEM((experts_dev, dat_count * cap_dev, units), bf16),
             pltpu.VMEM((slots, 1), f32),
             pltpu.VMEM((chunks, PAIR, PAIR, experts_dev, cap_dev, CHUNK), bf16),
@@ -392,7 +414,7 @@
         compiler_params=pltpu.CompilerParams(
             collective_id=0, has_side_effects=True, vmem_limit_bytes=60 * 1024 * 1024
         ),
-    )(tokens, norm_gain.reshape(1, width), router_weight, ids, inner_weight, outer_weight)
+    )(tokens, norm_gain.reshape(1, width), router_weight.T, slot_tokens, inner_weight, outer_weight)
 
 
 def solution(mesh):

time: 82.8 us -> 77.4 us (0.935)
  local copies, waits for them, and re-layouts: 4.6 us -> 1.67 us
  Pallas kernels: 77.9 us -> 75.6 us
    pallas_call x1, Pallas kernels: 77.9 us -> 75.6 us  [kernel_body(): pl.pallas_call(moe_kernel, out_shape=jax.ShapeDtypeStruct((tok_rows, widt...]
    unnamed x2 -> x1, local copies, waits for them, and re-layouts: 3.25 us -> 1.67 us
    broadcast_in_dim x2 -> x0, local copies, waits for them, and re-layouts: 1.36 us -> none  [kernel_body(): ids = jnp.broadcast_to(slot_tokens.reshape(1, slots), (8, slots))]
where the time goes in v2:
time: 77.4 us; the launch traced here: 77.3 us
  Pallas kernels  75.6 us (98%)
  local copies, waits for them, and re-layouts  1.67 us (2%)
    pallas_call x1, Pallas kernels, kernel_body(): pl.pallas_call(moe_kernel, out_shape=jax.ShapeDtypeStruct((tok_rows, widt...  75.6 us
    unnamed x1, local copies, waits for them, and re-layouts  1.67 us

profile of v2, /device:TPU:0, one launch (start us, length us, event | category | flops | bytes accessed | tf_op | source)
XLA Modules:
  0.0 77.3 jit_solution(5091043987613149511)
XLA Ops:
  0.0 75.6 %shard_map.64 = bf16[128,1024]{1,0:T(8,128)(2,1)} custom-call(bf16[128,1024]{1,0:T(8,128)(2,1)} %tokens_ref.1, f32[1,1024]{1,0:T(1,128)} %bitcast.3, bf16[4,1024]{1,0:T(4,128)(2,1)} %bitcast.2, s32[4,64]{1,0:T(4,128)} %ids_ref.1, bf16[4,1024,1024]{2,1,0:T(8,128)(2,1)} %inner_hbm.1, bf16[4,1024,1024]{2,1,0:T(8,128)(2,1)} %outer_hbm.1), custom_call_target="tpu_custom_call" | custom-call | tf_op jit(solution)/shard_map/pallas_call | solution.py:369
  75.6 1.7 %copy.8 = bf16[128,1024]{1,0:T(8,128)(2,1)} copy(bf16[128,1024]{1,0:T(8,128)(2,1)} %shard_map.64) | data formatting | bytes 524288
